TPU v7x, 256 devices: a whole 4x4x8 slice. The times are simulated.
256 devices in a mesh: pts: 64 (over z, x, core), poly: 4 (over y).
Axes of the slice: x: 4, y: 4, z: 8, core: 2. Of those that a mesh axis runs over, the one named last changes fastest.
Arguments:
- points: float32 [2, 524288], P(None, 'pts'), may hold values from 0 to 64, as said below
- segments: float32 [4, 8388608], P(None, ('pts', 'poly')), may hold values from -2.1 to 66.1, as said below
- edge_polygon: int32 [8388608], P(('pts', 'poly')), may hold values from 0 to 32767
- polygon_value: float32 [32768], replicated, may hold values from -6 to 6
- block_pairs: int32 [64, 3, 2, 8], P('pts'), may hold values from 0 to 127, as said below
- live_slots: int32 [64, 3], P('pts'), may hold values from 2 to 8, as said below
Outputs:
- min_sq: float32 [524288], P('pts')
- soft_label: float32 [524288], P('pts')
Inputs may be any that keep to these rules, and one draw needn't show every extreme that they name: `points`: point i lies in cell c = i // 8192: its x lies from c to c + 1, its y from 0 to 1. `segments`: edge e belongs to cell c = e // 131072: its start x lies from c - 2 to c + 3, its start y from 0 to 1, and its length from 0.02 to 0.1. block_pairs[c, r, 0, k] is a point block below 8; block_pairs[c, r, 1, k] is below 64 for r = 0 and below 128 otherwise, and the cell that it names always lies in the grid. For r >= 1, slot 0 names a block of cell c + r and slot 1 one of cell c - r wherever that cell lies in the grid. `live_slots`: at least two slots are used; in every cycle some cell uses all 8 slots.
All inputs are finite; a program needn't handle non-finite values.
Results may differ from a plain program's by a relative error of at most 0.0003.
Values sent between devices are 32-bit elements; how exact they have to be, the bound alone decides.
No kernel may reach another device: no remote copies, remote signals or barrier semaphores. Data moves between devices by JAX's collectives and lax.ppermute only.
A program may use at most 64 MiB of HBM per device.

v0:
```python
import math

import jax
import jax.numpy as jnp
from jax import lax
from jax.experimental import pallas as pl
from jax.experimental.pallas import tpu as pltpu
from jax.sharding import PartitionSpec as P


BP = 1024
BE = 512
EB = 64
SLOTS = 8
CUTOFF = 9.0
SCALE = 256.0 / 9.0 / math.log(2.0)
ROOT = math.sqrt(SCALE)
FAR = CUTOFF * SCALE
OFFSET = 110.0
SAFE = 200.0
UNSEEN = 1.0e30

SMEM = pl.BlockSpec(memory_space=pltpu.SMEM)
VMEM = pl.BlockSpec(memory_space=pltpu.VMEM)


def swapped(shard, axis, partner):
    devices = lax.axis_size(axis)
    pairs = [(i, partner(i)) for i in range(devices) if 0 <= partner(i) < devices]
    return lax.ppermute(shard, axis, pairs)


def pack_kernel(corners, polygons, out):
    out[0:1024, :] = corners[...]
    out[1024:1280, :] = polygons[...].astype(jnp.float32)


def packed_cell(segments, edge_polygon):
    corners = segments.reshape(4, -1, 128).transpose(1, 0, 2).reshape(-1, 128)
    return pl.pallas_call(
        pack_kernel,
        out_shape=jax.ShapeDtypeStruct((1280, 128), jnp.float32),
        in_specs=[VMEM] * 2,
        out_specs=VMEM,
        compiler_params=pltpu.CompilerParams(vmem_limit_bytes=4 << 20),
        cost_estimate=pl.CostEstimate(flops=1 << 20, bytes_accessed=1 << 21, transcendentals=0),
        name="pack",
    )(corners, edge_polygon.reshape(-1, 128))


def pieces(x):
    first = x.astype(jnp.bfloat16).astype(jnp.float32)
    rest = x - first
    second = rest.astype(jnp.bfloat16).astype(jnp.float32)
    return first, second, rest - second


def affine_rows(x_factor, y_factor, constant):
    x, y, c = pieces(x_factor), pieces(y_factor), pieces(constant)
    zero = jnp.zeros_like(x_factor)
    rows = [x[0], x[0], x[1], x[1], x[0], x[2], y[0], y[0], y[1], y[1], y[0], y[2], c[0], c[1], c[2], zero]
    return jnp.concatenate(rows, axis=0)


def squared_distance(u, v, half):
    beyond = jnp.maximum(jnp.abs(u) - half, 0.0)
    return v * v + beyond * beyond


TILES = BE // 128


def join_kernel(cycle, pairs, live, points, table, *refs):
    if cycle == 0:
        (near, out), scratch = refs[:2], refs[2:]
    else:
        (near, far, prior, out), scratch = refs[:4], refs[4:]
    raw, names, spots, table2, halves, left, right, column, spreader = scratch[:9]
    spread, even, odd, m_ref, s_ref, t_ref = scratch[9:]
    sub8 = lax.broadcasted_iota(jnp.int32, (8, 128), 0)
    total = live[0, cycle]

    for s in range(SLOTS):
        name = pairs[0, cycle, 1, s]
        block = name & (EB - 1)
        corner_rows = pl.ds(pl.multiple_of(16 * block, 16), 16)
        name_rows = pl.ds(1024 + 4 * block, 4)
        corner, polygon = near[corner_rows, :], near[name_rows, :]
        if cycle:
            below_is_near = (lax.axis_index("pts") & 1) == 1
            take_near = (name < EB) == below_is_near
            corner = jnp.where(take_near, corner, far[corner_rows, :])
            polygon = jnp.where(take_near, polygon, far[name_rows, :])
        raw[16 * s : 16 * s + 16, :] = corner
        names[8 * s : 8 * s + 4, :] = polygon
        names[8 * s + 4 : 8 * s + 8, :] = polygon

    for r in range(128):
        one = jnp.broadcast_to(table[r : r + 1, :], (8, 128))
        other = jnp.broadcast_to(table[r + 128 : r + 129, :], (8, 128))
        table2[8 * r : 8 * r + 8, :] = jnp.where(sub8 < 4, one, other)

    for i in range(64):
        for c in range(2):
            spots[3 * c, i : i + 1, :] = points[c : c + 1, 128 * i : 128 * (i + 1)]
    centre_x = points[0:1, 0:1]
    for c, centre in ((0, centre_x), (1, 0.5)):
        for i, piece in enumerate(pieces(spots[3 * c] - centre)):
            spots[3 * c + i] = piece

    for j in range(TILES):
        start_x, start_y, end_x, end_y = (
            raw[pl.ds(4 * j + c, SLOTS, stride=16), :] for c in range(4)
        )
        delta_x = end_x - start_x
        delta_y = end_y - start_y
        middle_x = (start_x - centre_x) + 0.5 * delta_x
        middle_y = (start_y - 0.5) + 0.5 * delta_y
        squared = jnp.maximum(delta_x * delta_x + delta_y * delta_y, 1e-12)
        inverse = lax.rsqrt(squared) * ROOT
        along_x = delta_x * inverse
        along_y = delta_y * inverse
        halves[8 * j : 8 * j + 8, :] = 0.5 * squared * inverse
        along = affine_rows(along_x, along_y, -(middle_x * along_x + middle_y * along_y))
        across = affine_rows(-along_y, along_x, middle_x * along_y - middle_y * along_x)
        left[128 * j : 128 * (j + 1), :] = along.T.astype(jnp.bfloat16)
        left[BE + 128 * j : BE + 128 * (j + 1), :] = across.T.astype(jnp.bfloat16)

    row = lax.broadcasted_iota(jnp.int32, (128, 256), 0)
    lane = lax.broadcasted_iota(jnp.int32, (128, 256), 1)
    first = jnp.where(lane < 128, 24, 0)
    for j in range(TILES):
        inside = (row >= first) & (row < first + 24) & ((row & 7) == j)
        spreader[j] = jnp.where(inside, 1.0, 0.0).astype(jnp.bfloat16)

    m_ref[...] = jnp.full_like(m_ref, UNSEEN)
    s_ref[...] = jnp.zeros_like(s_ref)
    t_ref[...] = jnp.zeros_like(t_ref)

    def block_of(q):
        return pairs[0, cycle, 0, q]

    def look_up(q):
        index = names[pl.ds(pl.multiple_of(8 * q, 8), 8), :].astype(jnp.int32)
        low = index & 127
        high = index >> 7
        bits = [((high >> b) & 1) == 1 for b in range(7)]

        def found(r, b):
            if b < 0:
                part = table2[8 * r : 8 * r + 8, :]
                return jnp.take_along_axis(part, low, axis=1, mode="promise_in_bounds")
            return jnp.where(bits[b], found(r + (1 << b), b - 1), found(r, b - 1))

        both = found(0, 6)
        return jnp.where(high >= 128, pltpu.roll(both, 4, 0), both)

    def set_right(q):
        p = block_of(q)
        here = sub8 == q
        zero = jnp.zeros((8, 128), jnp.float32)
        one = jnp.where(here, 1.0, 0.0)
        for n in range(8):
            at = pl.ds(8 * p + n, 1)
            part = [
                jnp.where(here, jnp.broadcast_to(spots[i, at, :], (8, 128)), 0.0) for i in range(6)
            ]
            x, y = part[:3], part[3:]
            rows = []
            for c in (x, y):
                rows += [c[0], c[1], c[0], c[1], c[2], c[0]]
            rows += [one, one, one, zero]
            right[:, 128 * n : 128 * (n + 1)] = jnp.concatenate(rows, axis=0).astype(jnp.bfloat16)

    def set_column(q):
        half = jnp.concatenate(
            [halves[pl.ds(8 * j + q, 1), :] for j in range(TILES)]
            + [jnp.zeros((8 - TILES, 128), jnp.float32)],
            axis=0,
        )
        rows = list(pieces(look_up(q))) + list(pieces(half))
        full = jnp.concatenate(rows + [jnp.zeros((80, 128), jnp.float32)], axis=0)
        column[...] = full.T.astype(jnp.bfloat16)

    def multiply(n, buf):
        buf[...] = jnp.dot(
            left[...], right[:, 256 * n : 256 * (n + 1)], preferred_element_type=jnp.float32
        )

    def set_spread():
        for j in range(TILES):
            spread[128 * j : 128 * (j + 1), :] = jnp.dot(
                column[...], spreader[j], preferred_element_type=jnp.float32
            )

    def add_up(p, n, buf):
        m, s, t = [None, None], [None, None], [None, None]
        for g in range(BE // 8):
            up, down = slice(8 * g, 8 * g + 8), slice(BE + 8 * g, BE + 8 * g + 8)
            half = spread[up, 0:128]
            value = spread[up, 128:256]
            for h in range(2):
                at = slice(128 * h, 128 * (h + 1))
                d = squared_distance(buf[up, at], buf[down, at], half)
                w = jnp.exp2(OFFSET - d)
                m[h] = jnp.minimum(m[h], d) if g else d
                s[h] = s[h] + w if g else w
                t[h] = t[h] + w * value if g else w * value
        for h in range(2):
            here = pl.ds(8 * p + (2 * n + h), 1)
            m_ref[here, :] = jnp.minimum(m_ref[here, :], jnp.min(m[h], axis=0, keepdims=True))
            s_ref[here, :] = s_ref[here, :] + jnp.sum(s[h], axis=0, keepdims=True)
            t_ref[here, :] = t_ref[here, :] + jnp.sum(t[h], axis=0, keepdims=True)

    set_right(0)
    multiply(0, even)
    set_column(0)
    set_spread()

    def slot(q, carry):
        p = block_of(q)
        later = jnp.minimum(q + 1, total - 1)
        multiply(1, odd)
        add_up(p, 0, even)
        multiply(2, even)
        add_up(p, 1, odd)
        multiply(3, odd)
        add_up(p, 2, even)
        set_right(later)
        set_column(later)
        multiply(0, even)
        add_up(p, 3, odd)
        set_spread()
        return carry

    lax.fori_loop(0, total, slot, 0)

    def finish(*result):
        if cycle:
            result = combine(result, unpack(prior))
        for i, part in enumerate(result):
            out[64 * i : 64 * (i + 1), :] = part

    m = m_ref[...]
    seen = m < 0.5 * UNSEEN
    unsafe = jnp.max(jnp.where(seen & (m > SAFE), 1.0, 0.0)) > 0.0
    back = jnp.exp2(jnp.where(seen, m, OFFSET) - OFFSET)
    finish(jnp.where(seen, m, FAR), s_ref[...] * back, t_ref[...] * back)

    @pl.when(unsafe)
    def _():
        m_ref[...] = jnp.full_like(m_ref, FAR)
        s_ref[...] = jnp.zeros_like(s_ref)
        t_ref[...] = jnp.zeros_like(t_ref)

        def far_slot(q, carry):
            set_right(q)
            set_column(q)
            set_spread()
            for n in range(4):
                multiply(n, even)
                for h in range(2):
                    at = slice(128 * h, 128 * (h + 1))

                    def terms(g):
                        up = pl.ds(pl.multiple_of(8 * g, 8), 8)
                        down = pl.ds(pl.multiple_of(BE + 8 * g, 8), 8)
                        d = squared_distance(even[up, at], even[down, at], spread[up, 0:128])
                        return d, spread[up, 128:256]

                    def lower(g, m):
                        return jnp.minimum(m, terms(g)[0])

                    least = jnp.full((8, 128), UNSEEN, jnp.float32)
                    least = lax.fori_loop(0, BE // 8, lower, least)
                    least = jnp.min(least, axis=0, keepdims=True)

                    def add(g, sums):
                        d, value = terms(g)
                        w = jnp.exp2(least - d)
                        return sums[0] + w, sums[1] + w * value

                    zero = jnp.zeros((8, 128), jnp.float32)
                    sums = lax.fori_loop(0, BE // 8, add, (zero, zero))
                    new = (least, *(jnp.sum(x, axis=0, keepdims=True) for x in sums))
                    here = pl.ds(8 * block_of(q) + (2 * n + h), 1)
                    old = (m_ref[here, :], s_ref[here, :], t_ref[here, :])
                    m_ref[here, :], s_ref[here, :], t_ref[here, :] = combine(old, new)
            return carry

        lax.fori_loop(0, total, far_slot, 0)
        finish(m_ref[...], s_ref[...], t_ref[...])


def join(cycle, block_pairs, live_slots, points, table, *sources):
    body = lambda *refs: join_kernel(cycle, *refs)
    bf16, f32 = jnp.bfloat16, jnp.float32
    pairs = 8.0 * BP * BE
    return pl.pallas_call(
        body,
        out_shape=jax.ShapeDtypeStruct((192, 128), f32),
        in_specs=[SMEM] * 2 + [VMEM] * (2 + len(sources)),
        out_specs=VMEM,
        scratch_shapes=[
            pltpu.VMEM((16 * SLOTS, 128), f32),
            pltpu.VMEM((8 * SLOTS, 128), f32),
            pltpu.VMEM((6, 64, 128), f32),
            pltpu.VMEM((1024, 128), f32),
            pltpu.VMEM((32, 128), f32),
            pltpu.VMEM((2 * BE, 128), bf16),
            pltpu.VMEM((128, BP), bf16),
            pltpu.VMEM((128, 128), bf16),
            pltpu.VMEM((TILES, 128, 256), bf16),
        ]
        + [pltpu.VMEM((BE, 256), f32)]
        + [pltpu.VMEM((2 * BE, 256), f32)] * 2
        + [pltpu.VMEM((64, 128), f32)] * 3,
        compiler_params=pltpu.CompilerParams(vmem_limit_bytes=40 << 20),
        cost_estimate=pl.CostEstimate(
            flops=int(20 * pairs), bytes_accessed=1 << 20, transcendentals=int(pairs)
        ),
    )(block_pairs, live_slots, points, table, *sources)


def combine(one, other):
    least = jnp.minimum(one[0], other[0])
    share = jnp.exp2(least - one[0])
    other_share = jnp.exp2(least - other[0])
    return (
        least,
        one[1] * share + other[1] * other_share,
        one[2] * share + other[2] * other_share,
    )


def unpack(state):
    return state[0:64, :], state[64:128, :], state[128:192, :]


def steps(points, segments, edge_polygon, polygon_value, block_pairs, live_slots):
    mine = packed_cell(segments, edge_polygon)
    inner = lambda shard: swapped(shard, "pts", lambda c: c ^ 1)
    outer = lambda shard: swapped(shard, "pts", lambda c: ((c + 1) ^ 1) - 1)
    args = (block_pairs, live_slots, points, polygon_value.reshape(-1, 128))
    near1 = inner(mine)
    far1 = outer(mine)
    far2 = outer(near1)
    part = join(0, *args, mine)
    far1, part = lax.optimization_barrier((far1, part))
    near2 = inner(far1)
    part = join(1, *args, near1, far1, part)
    part = join(2, *args, near2, far2, part)
    state = unpack(part)
    for flip in (1, 3, 2):
        state = combine(state, unpack(swapped(part, "poly", lambda q: q ^ flip)))
    state = combine(state, (FAR, 1.0, 0.0))
    return (state[0] * (1.0 / SCALE)).reshape(-1), (state[2] / state[1]).reshape(-1)


def solution(mesh):
    placed = (
        P(None, "pts"),
        P(None, ("pts", "poly")),
        P(("pts", "poly")),
        P(),
        P("pts", None, None, None),
        P("pts", None),
    )
    return jax.shard_map(
        steps, mesh=mesh, in_specs=placed, out_specs=(P("pts"), P("pts")), check_vma=False
    )
```

profile of v0, /device:TPU:128, one launch (start us, length us, event | category | flops | bytes accessed | tf_op | source)
XLA Modules:
  0.0 53.1 jit_solution(13410766318272196566)
XLA Ops:
  0.6 0.0 copy-start
  0.6 1.0 %copy-done = f32[4,32768]{1,0:T(4,128)S(1)} copy-done((f32[4,32768]{1,0:T(4,128)S(1)}, f32[4,32768]{1,0:T(4,128)}, u32[]{:S(2)}) %copy-start) | copy-done | bytes 524312
  1.7 0.0 copy-start.1
  1.7 0.9 %copy-done.1 = s32[32768]{0:T(1024)S(1)} copy-done((s32[32768]{0:T(1024)S(1)}, s32[32768]{0:T(1024)}, u32[]{:S(2)}) %copy-start.1) | copy-done | bytes 131096
  2.6 0.0 copy-start.2
  2.6 0.0 copy-start.3
  2.6 0.0 copy-start.4
  2.6 0.0 copy-start.5
  2.6 3.8 %collective-permute-start = (f32[1280,128]{1,0:T(8,128)S(1)}, f32[1280,128]{1,0:T(8,128)S(1)}, u32[]{:S(2)}, u32[]{:S(2)}) collective-permute-start(f32[1280,128]{1,0:T(8,128)S(1)} %pack.1.refs_4_), channel_id=1, source_target_pairs={{4,8},{8,4},{12,16},{16,12},{20,24},{24,20},{28,32},{32,28},{36,40... | collective-permute-start | bytes 1966088 | tf_op jit(solution)/shard_map/ppermute | solution.py:30
  6.4 0.1 collective-permute-start.2
  6.5 0.0 copy-done.2
  6.5 0.0 copy-done.3
  6.6 0.0 copy-done.4
  6.6 0.0 copy-done.5
  6.6 7.1 %shard_map.77.refs_6_ = f32[192,128]{1,0:T(8,128)S(1)} custom-call(s32[1,3,2,8]{3,2,1,0:T(2,128)S(1)} %copy-done.4, s32[1,3]{1,0:T(1,128)S(1)} %copy-done.5, f32[2,8192]{1,0:T(2,128)S(1)} %copy-done.3, f32[256,128]{1,0:T(8,128)S(1)} %bitcast.13, f32[1280,128]{1,0:T(8,128)S(1)} %pack.1.refs_4_), custom_call_target="tpu_custom_call" | custom-call | flops 83886080 | bytes 1048576 | tf_op jit(solution)/shard_map/pallas_call | solution.py:299
  13.7 4.3 %collective-permute-done.refs_5_ = f32[1280,128]{1,0:T(8,128)S(1)} collective-permute-done((f32[1280,128]{1,0:T(8,128)S(1)}, f32[1280,128]{1,0:T(8,128)S(1)}, u32[]{:S(2)}, u32[]{:S(2)}) %collective-permute-start) | collective-permute-done | bytes 655392 | tf_op jit(solution)/shard_map/ppermute | solution.py:30
  18.0 0.0 collective-permute-start.1
  18.0 0.0 collective-permute-done.2.refs_4_
  18.0 3.6 %collective-permute-start.3 = (f32[1280,128]{1,0:T(8,128)S(1)}, f32[1280,128]{1,0:T(8,128)S(1)}, u32[]{:S(2)}, u32[]{:S(2)}) collective-permute-start(f32[1280,128]{1,0:T(8,128)S(1)} %collective-permute-done.2.refs_4_), channel_id=1, source_target_pairs={{4,8},{8,4},{12,16},{16,12},{20,24},{24,20},{28,32},{32,28},{36,40... | collective-permute-start | bytes 1966088 | tf_op jit(solution)/shard_map/ppermute | solution.py:30
  21.7 7.0 %shard_map.78.refs_6_ = f32[192,128]{1,0:T(8,128)S(1)} custom-call(s32[1,3,2,8]{3,2,1,0:T(2,128)S(1)} %copy-done.4, s32[1,3]{1,0:T(1,128)S(1)} %copy-done.5, f32[2,8192]{1,0:T(2,128)S(1)} %copy-done.3, f32[256,128]{1,0:T(8,128)S(1)} %bitcast.14, f32[1280,128]{1,0:T(8,128)S(1)} %collective-permute-done.2.refs_4_, ...), custom_call_target="tpu_custom_call" | custom-call | flops 83886080 | bytes 1048576 | tf_op jit(solution)/shard_map/pallas_call | solution.py:299
  28.7 0.0 collective-permute-done.1.refs_4_
  28.7 4.5 %collective-permute-done.3.refs_5_ = f32[1280,128]{1,0:T(8,128)S(1)} collective-permute-done((f32[1280,128]{1,0:T(8,128)S(1)}, f32[1280,128]{1,0:T(8,128)S(1)}, u32[]{:S(2)}, u32[]{:S(2)}) %collective-permute-start.3) | collective-permute-done | bytes 655392 | tf_op jit(solution)/shard_map/ppermute | solution.py:30
  33.2 9.2 %shard_map.79 = f32[192,128]{1,0:T(8,128)S(1)} custom-call(s32[1,3,2,8]{3,2,1,0:T(2,128)S(1)} %copy-done.4, s32[1,3]{1,0:T(1,128)S(1)} %copy-done.5, f32[2,8192]{1,0:T(2,128)S(1)} %copy-done.3, f32[256,128]{1,0:T(8,128)S(1)} %bitcast.15, f32[1280,128]{1,0:T(8,128)S(1)} %collective-permute-done.1.refs_4_, f32[1280,128]{1,0:T(8,128)S(1)} %collective-permute-done.3.refs_5_, ...), custom_call_target="tpu_custom_call" | custom-call | flops 83886080 | bytes 1048576 | tf_op jit(solution)/shard_map/pallas_call | solution.py:299
  42.5 1.7 %collective-permute-start.4 = (f32[192,128]{1,0:T(8,128)S(1)}, f32[192,128]{1,0:T(8,128)S(1)}, u32[]{:S(2)}, u32[]{:S(2)}) collective-permute-start(f32[192,128]{1,0:T(8,128)S(1)} %shard_map.79), channel_id=1, source_target_pairs={{0,1},{1,0},{2,3},{3,2},{4,5},{5,4},{6,7},{7,6},{8,9},{9,8},{10,11... | collective-permute-start | bytes 294920 | tf_op jit(solution)/shard_map/ppermute | solution.py:30
  44.1 2.2 %collective-permute-start.5 = (f32[192,128]{1,0:T(8,128)S(1)}, f32[192,128]{1,0:T(8,128)S(1)}, u32[]{:S(2)}, u32[]{:S(2)}) collective-permute-start(f32[192,128]{1,0:T(8,128)S(1)} %shard_map.79), channel_id=1, source_target_pairs={{0,3},{1,2},{2,1},{3,0},{4,7},{5,6},{6,5},{7,4},{8,11},{9,10},{10,... | collective-permute-start | bytes 294920 | tf_op jit(solution)/shard_map/ppermute | solution.py:30
  46.3 0.7 %collective-permute-start.6 = (f32[192,128]{1,0:T(8,128)S(1)}, f32[192,128]{1,0:T(8,128)S(1)}, u32[]{:S(2)}, u32[]{:S(2)}) collective-permute-start(f32[192,128]{1,0:T(8,128)S(1)} %shard_map.79), channel_id=1, source_target_pairs={{0,2},{1,3},{2,0},{3,1},{4,6},{5,7},{6,4},{7,5},{8,10},{9,11},{10,... | collective-permute-start | bytes 294920 | tf_op jit(solution)/shard_map/ppermute | solution.py:30
  47.0 0.1 collective-permute-done.4
  47.2 2.8 %collective-permute-done.5 = f32[192,128]{1,0:T(8,128)S(1)} collective-permute-done((f32[192,128]{1,0:T(8,128)S(1)}, f32[192,128]{1,0:T(8,128)S(1)}, u32[]{:S(2)}, u32[]{:S(2)}) %collective-permute-start.5) | collective-permute-done | bytes 98336 | tf_op jit(solution)/shard_map/ppermute | solution.py:30
  50.0 2.5 %collective-permute-done.6 = f32[192,128]{1,0:T(8,128)S(1)} collective-permute-done((f32[192,128]{1,0:T(8,128)S(1)}, f32[192,128]{1,0:T(8,128)S(1)}, u32[]{:S(2)}, u32[]{:S(2)}) %collective-permute-start.6) | collective-permute-done | bytes 98336 | tf_op jit(solution)/shard_map/ppermute | solution.py:30
  52.4 0.7 %fusion.9 = (f32[8192]{0:T(1024)}, f32[8192]{0:T(1024)}) fusion(f32[192,128]{1,0:T(8,128)S(1)} %collective-permute-done.6, f32[192,128]{1,0:T(8,128)S(1)} %collective-permute-done.5, f32[192,128]{1,0:T(8,128)S(1)} %collective-permute-done.4, f32[192,128]{1,0:T(8,128)S(1)} %shard_map.79), kind=kLoop, calls=%fused_computation.13 | loop fusion | flops 368640 | bytes 458752 | tf_op jit(solution)/shard_map/reshape | solution.py:357
  (1 shorter events, 0.0 us)
Async XLA Ops:
  0.6 1.0 %copy-start = (f32[4,32768]{1,0:T(4,128)S(1)}, f32[4,32768]{1,0:T(4,128)}, u32[]{:S(2)}) copy-start(f32[4,32768]{1,0:T(4,128)} %param.7) | copy-start | bytes 1572868
  1.7 0.9 %copy-start.1 = (s32[32768]{0:T(1024)S(1)}, s32[32768]{0:T(1024)}, u32[]{:S(2)}) copy-start(s32[32768]{0:T(1024)} %param.8) | copy-start | bytes 393220
  2.6 4.0 %copy-start.2 = (f32[32768]{0:T(1024)S(1)}, f32[32768]{0:T(1024)}, u32[]{:S(2)}) copy-start(f32[32768]{0:T(1024)} %param.9) | copy-start | bytes 393220
  2.6 4.0 %copy-start.3 = (f32[2,8192]{1,0:T(2,128)S(1)}, f32[2,8192]{1,0:T(2,128)}, u32[]{:S(2)}) copy-start(f32[2,8192]{1,0:T(2,128)} %refs_2_.5) | copy-start | bytes 196612
  2.6 4.0 %copy-start.4 = (s32[1,3,2,8]{3,2,1,0:T(2,128)S(1)}, s32[1,3,2,8]{3,2,1,0:T(2,128)}, u32[]{:S(2)}) copy-start(s32[1,3,2,8]{3,2,1,0:T(2,128)} %refs_0_.5) | copy-start | bytes 580
  2.6 3.9 %copy-start.5 = (s32[1,3]{1,0:T(1,128)S(1)}, s32[1,3]{1,0:T(1,128)}, u32[]{:S(2)}) copy-start(s32[1,3]{1,0:T(1,128)} %refs_1_.5) | copy-start | bytes 40
  2.6 15.4 %collective-permute-start = (f32[1280,128]{1,0:T(8,128)S(1)}, f32[1280,128]{1,0:T(8,128)S(1)}, u32[]{:S(2)}, u32[]{:S(2)}) collective-permute-start(f32[1280,128]{1,0:T(8,128)S(1)} %pack.1.refs_4_), channel_id=1, source_target_pairs={{4,8},{8,4},{12,16},{16,12},{20,24},{24,20},{28,32},{32,28},{36,40... | collective-permute-start | bytes 1966088 | tf_op jit(solution)/shard_map/ppermute | solution.py:30
  6.4 11.6 %collective-permute-start.2 = (f32[1280,128]{1,0:T(8,128)S(1)}, f32[1280,128]{1,0:T(8,128)S(1)}, u32[]{:S(2)}, u32[]{:S(2)}) collective-permute-start(f32[1280,128]{1,0:T(8,128)S(1)} %pack.1.refs_4_), channel_id=1, source_target_pairs={{0,4},{4,0},{8,12},{12,8},{16,20},{20,16},{24,28},{28,24},{32,36},... | collective-permute-start | bytes 1966088 | tf_op jit(solution)/shard_map/ppermute | solution.py:30
  18.0 10.7 %collective-permute-start.1 = (f32[1280,128]{1,0:T(8,128)S(1)}, f32[1280,128]{1,0:T(8,128)S(1)}, u32[]{:S(2)}, u32[]{:S(2)}) collective-permute-start(f32[1280,128]{1,0:T(8,128)S(1)} %collective-permute-done.refs_5_), channel_id=1, source_target_pairs={{0,4},{4,0},{8,12},{12,8},{16,20},{20,16},{24,28},{28,24},{32,36},... | collective-permute-start | bytes 1966088 | tf_op jit(solution)/shard_map/ppermute | solution.py:30
  18.0 15.2 %collective-permute-start.3 = (f32[1280,128]{1,0:T(8,128)S(1)}, f32[1280,128]{1,0:T(8,128)S(1)}, u32[]{:S(2)}, u32[]{:S(2)}) collective-permute-start(f32[1280,128]{1,0:T(8,128)S(1)} %collective-permute-done.2.refs_4_), channel_id=1, source_target_pairs={{4,8},{8,4},{12,16},{16,12},{20,24},{24,20},{28,32},{32,28},{36,40... | collective-permute-start | bytes 1966088 | tf_op jit(solution)/shard_map/ppermute | solution.py:30
  42.5 4.7 %collective-permute-start.4 = (f32[192,128]{1,0:T(8,128)S(1)}, f32[192,128]{1,0:T(8,128)S(1)}, u32[]{:S(2)}, u32[]{:S(2)}) collective-permute-start(f32[192,128]{1,0:T(8,128)S(1)} %shard_map.79), channel_id=1, source_target_pairs={{0,1},{1,0},{2,3},{3,2},{4,5},{5,4},{6,7},{7,6},{8,9},{9,8},{10,11... | collective-permute-start | bytes 294920 | tf_op jit(solution)/shard_map/ppermute | solution.py:30
  44.1 5.8 %collective-permute-start.5 = (f32[192,128]{1,0:T(8,128)S(1)}, f32[192,128]{1,0:T(8,128)S(1)}, u32[]{:S(2)}, u32[]{:S(2)}) collective-permute-start(f32[192,128]{1,0:T(8,128)S(1)} %shard_map.79), channel_id=1, source_target_pairs={{0,3},{1,2},{2,1},{3,0},{4,7},{5,6},{6,5},{7,4},{8,11},{9,10},{10,... | collective-permute-start | bytes 294920 | tf_op jit(solution)/shard_map/ppermute | solution.py:30
  46.3 6.1 %collective-permute-start.6 = (f32[192,128]{1,0:T(8,128)S(1)}, f32[192,128]{1,0:T(8,128)S(1)}, u32[]{:S(2)}, u32[]{:S(2)}) collective-permute-start(f32[192,128]{1,0:T(8,128)S(1)} %shard_map.79), channel_id=1, source_target_pairs={{0,2},{1,3},{2,0},{3,1},{4,6},{5,7},{6,4},{7,5},{8,10},{9,11},{10,... | collective-permute-start | bytes 294920 | tf_op jit(solution)/shard_map/ppermute | solution.py:30
where the time goes:
time: 53.3 us; the launch traced here: 53.1 us
  Pallas kernels  23.4 us (44%)
  waiting for transfers between devices  14.2 us (27%)
  starting transfers between devices  12.1 us (23%)
  local copies, waits for them, and re-layouts  1.96 us (4%)
  between operations  0.75 us (1%)
  other arithmetic  0.7 us (1%)
    pallas_call x3, Pallas kernels, join(): pl.pallas_call(body, out_shape=jax.ShapeDtypeStruct((192, 128), f32), in_...  23.3 us
    ppermute x7, waiting for transfers between devices, swapped(): return lax.ppermute(shard, axis, pairs)  14.2 us
    ppermute x7, starting transfers between devices, swapped(): return lax.ppermute(shard, axis, pairs)  12.1 us
    unnamed x12, local copies, waits for them, and re-layouts  1.96 us
  transfers between devices with their start and end apart: 7, of which 5 were waited for; matrix products, arithmetic and copies ran while one was open for 0% of the time, Pallas kernels for 27%

commit v1 on v0

--- a/solution.py
+++ b/solution.py
@@ -76,7 +76,7 @@
     else:
         (near, far, prior, out), scratch = refs[:4], refs[4:]
     raw, names, spots, table2, halves, left, right, column, spreader = scratch[:9]
-    spread, even, odd, m_ref, s_ref, t_ref = scratch[9:]
+    spread, even, m_ref, s_ref, t_ref = scratch[9:]
     sub8 = lax.broadcasted_iota(jnp.int32, (8, 128), 0)
     total = live[0, cycle]
 
@@ -182,8 +182,8 @@
         full = jnp.concatenate(rows + [jnp.zeros((80, 128), jnp.float32)], axis=0)
         column[...] = full.T.astype(jnp.bfloat16)
 
-    def multiply(n, buf):
-        buf[...] = jnp.dot(
+    def multiply(n):
+        return jnp.dot(
             left[...], right[:, 256 * n : 256 * (n + 1)], preferred_element_type=jnp.float32
         )
 
@@ -213,23 +213,23 @@
             t_ref[here, :] = t_ref[here, :] + jnp.sum(t[h], axis=0, keepdims=True)
 
     set_right(0)
-    multiply(0, even)
+    even[...] = multiply(0)
     set_column(0)
     set_spread()
 
     def slot(q, carry):
         p = block_of(q)
         later = jnp.minimum(q + 1, total - 1)
-        multiply(1, odd)
+        one = multiply(1)
         add_up(p, 0, even)
-        multiply(2, even)
-        add_up(p, 1, odd)
-        multiply(3, odd)
-        add_up(p, 2, even)
+        two = multiply(2)
+        add_up(p, 1, one)
+        three = multiply(3)
+        add_up(p, 2, two)
         set_right(later)
         set_column(later)
-        multiply(0, even)
-        add_up(p, 3, odd)
+        even[...] = multiply(0)
+        add_up(p, 3, three)
         set_spread()
         return carry
 
@@ -258,7 +258,7 @@
             set_column(q)
             set_spread()
             for n in range(4):
-                multiply(n, even)
+                even[...] = multiply(n)
                 for h in range(2):
                     at = slice(128 * h, 128 * (h + 1))
 
@@ -313,7 +313,7 @@
             pltpu.VMEM((TILES, 128, 256), bf16),
         ]
         + [pltpu.VMEM((BE, 256), f32)]
-        + [pltpu.VMEM((2 * BE, 256), f32)] * 2
+        + [pltpu.VMEM((2 * BE, 256), f32)]
         + [pltpu.VMEM((64, 128), f32)] * 3,
         compiler_params=pltpu.CompilerParams(vmem_limit_bytes=40 << 20),
         cost_estimate=pl.CostEstimate(
@@ -351,8 +351,9 @@
     part = join(1, *args, near1, far1, part)
     part = join(2, *args, near2, far2, part)
     state = unpack(part)
-    for flip in (1, 3, 2):
-        state = combine(state, unpack(swapped(part, "poly", lambda q: q ^ flip)))
+    for flip in (2, 3, 1):
+        theirs = swapped(part, "poly", lambda q: q ^ flip)
+        state = combine(state, unpack(theirs))
     state = combine(state, (FAR, 1.0, 0.0))
     return (state[0] * (1.0 / SCALE)).reshape(-1), (state[2] / state[1]).reshape(-1)
 

time: 53.3 us -> 52.7 us (0.989)
  waiting for transfers between devices: 14.2 us -> 13.2 us
  Pallas kernels: 23.4 us -> 24 us
    ppermute x7, waiting for transfers between devices: 14.2 us -> 13.2 us  [swapped(): return lax.ppermute(shard, axis, pairs)]
    pallas_call x3, Pallas kernels: 23.3 us -> 24 us  [join(): pl.pallas_call(body, out_shape=jax.ShapeDtypeStruct((192, 128), f32), in_...]
  transfers between devices with their start and end apart: 7 -> 7, of which waited for: 5 -> 4; matrix products, arithmetic and copies ran while one was open for 0% -> 0% of each run, Pallas kernels for 27% -> 28%
where the time goes in v1:
time: 52.7 us; the launch traced here: 52.5 us
  Pallas kernels  24 us (46%)
  waiting for transfers between devices  13.2 us (25%)
  starting transfers between devices  11.9 us (23%)
  local copies, waits for them, and re-layouts  1.96 us (4%)
  between operations  0.75 us (1%)
  other arithmetic  0.7 us (1%)
    pallas_call x3, Pallas kernels, join(): pl.pallas_call(body, out_shape=jax.ShapeDtypeStruct((192, 128), f32), in_...  24 us
    ppermute x7, waiting for transfers between devices, swapped(): return lax.ppermute(shard, axis, pairs)  13.2 us
    ppermute x7, starting transfers between devices, swapped(): return lax.ppermute(shard, axis, pairs)  11.9 us
    unnamed x12, local copies, waits for them, and re-layouts  1.96 us
  transfers between devices with their start and end apart: 7, of which 4 were waited for; matrix products, arithmetic and copies ran while one was open for 0% of the time, Pallas kernels for 28%

profile of v1, /device:TPU:128, one launch (start us, length us, event | category | flops | bytes accessed | tf_op | source)
XLA Modules:
  0.0 52.5 jit_solution(14826569770757378372)
XLA Ops:
  0.6 0.0 copy-start
  0.6 1.0 %copy-done = f32[4,32768]{1,0:T(4,128)S(1)} copy-done((f32[4,32768]{1,0:T(4,128)S(1)}, f32[4,32768]{1,0:T(4,128)}, u32[]{:S(2)}) %copy-start) | copy-done | bytes 524312
  1.7 0.0 copy-start.1
  1.7 0.9 %copy-done.1 = s32[32768]{0:T(1024)S(1)} copy-done((s32[32768]{0:T(1024)S(1)}, s32[32768]{0:T(1024)}, u32[]{:S(2)}) %copy-start.1) | copy-done | bytes 131096
  2.6 0.0 copy-start.2
  2.6 0.0 copy-start.3
  2.6 0.0 copy-start.4
  2.6 0.0 copy-start.5
  2.6 3.8 %collective-permute-start = (f32[1280,128]{1,0:T(8,128)S(1)}, f32[1280,128]{1,0:T(8,128)S(1)}, u32[]{:S(2)}, u32[]{:S(2)}) collective-permute-start(f32[1280,128]{1,0:T(8,128)S(1)} %pack.1.refs_4_), channel_id=1, source_target_pairs={{4,8},{8,4},{12,16},{16,12},{20,24},{24,20},{28,32},{32,28},{36,40... | collective-permute-start | bytes 1966088 | tf_op jit(solution)/shard_map/ppermute | solution.py:30
  6.4 0.1 collective-permute-start.2
  6.5 0.0 copy-done.2
  6.5 0.0 copy-done.3
  6.6 0.0 copy-done.4
  6.6 0.0 copy-done.5
  6.6 7.3 %shard_map.77.refs_6_ = f32[192,128]{1,0:T(8,128)S(1)} custom-call(s32[1,3,2,8]{3,2,1,0:T(2,128)S(1)} %copy-done.4, s32[1,3]{1,0:T(1,128)S(1)} %copy-done.5, f32[2,8192]{1,0:T(2,128)S(1)} %copy-done.3, f32[256,128]{1,0:T(8,128)S(1)} %bitcast.13, f32[1280,128]{1,0:T(8,128)S(1)} %pack.1.refs_4_), custom_call_target="tpu_custom_call" | custom-call | flops 83886080 | bytes 1048576 | tf_op jit(solution)/shard_map/pallas_call | solution.py:299
  13.9 4.1 %collective-permute-done.refs_5_ = f32[1280,128]{1,0:T(8,128)S(1)} collective-permute-done((f32[1280,128]{1,0:T(8,128)S(1)}, f32[1280,128]{1,0:T(8,128)S(1)}, u32[]{:S(2)}, u32[]{:S(2)}) %collective-permute-start) | collective-permute-done | bytes 655392 | tf_op jit(solution)/shard_map/ppermute | solution.py:30
  18.0 0.0 collective-permute-start.1
  18.0 0.0 collective-permute-done.2.refs_4_
  18.0 3.6 %collective-permute-start.3 = (f32[1280,128]{1,0:T(8,128)S(1)}, f32[1280,128]{1,0:T(8,128)S(1)}, u32[]{:S(2)}, u32[]{:S(2)}) collective-permute-start(f32[1280,128]{1,0:T(8,128)S(1)} %collective-permute-done.2.refs_4_), channel_id=1, source_target_pairs={{4,8},{8,4},{12,16},{16,12},{20,24},{24,20},{28,32},{32,28},{36,40... | collective-permute-start | bytes 1966088 | tf_op jit(solution)/shard_map/ppermute | solution.py:30
  21.7 7.2 %shard_map.78.refs_6_ = f32[192,128]{1,0:T(8,128)S(1)} custom-call(s32[1,3,2,8]{3,2,1,0:T(2,128)S(1)} %copy-done.4, s32[1,3]{1,0:T(1,128)S(1)} %copy-done.5, f32[2,8192]{1,0:T(2,128)S(1)} %copy-done.3, f32[256,128]{1,0:T(8,128)S(1)} %bitcast.14, f32[1280,128]{1,0:T(8,128)S(1)} %collective-permute-done.2.refs_4_, ...), custom_call_target="tpu_custom_call" | custom-call | flops 83886080 | bytes 1048576 | tf_op jit(solution)/shard_map/pallas_call | solution.py:299
  28.9 0.0 collective-permute-done.1.refs_4_
  28.9 4.3 %collective-permute-done.3.refs_5_ = f32[1280,128]{1,0:T(8,128)S(1)} collective-permute-done((f32[1280,128]{1,0:T(8,128)S(1)}, f32[1280,128]{1,0:T(8,128)S(1)}, u32[]{:S(2)}, u32[]{:S(2)}) %collective-permute-start.3) | collective-permute-done | bytes 655392 | tf_op jit(solution)/shard_map/ppermute | solution.py:30
  33.2 9.5 %shard_map.79 = f32[192,128]{1,0:T(8,128)S(1)} custom-call(s32[1,3,2,8]{3,2,1,0:T(2,128)S(1)} %copy-done.4, s32[1,3]{1,0:T(1,128)S(1)} %copy-done.5, f32[2,8192]{1,0:T(2,128)S(1)} %copy-done.3, f32[256,128]{1,0:T(8,128)S(1)} %bitcast.15, f32[1280,128]{1,0:T(8,128)S(1)} %collective-permute-done.1.refs_4_, f32[1280,128]{1,0:T(8,128)S(1)} %collective-permute-done.3.refs_5_, ...), custom_call_target="tpu_custom_call" | custom-call | flops 83886080 | bytes 1048576 | tf_op jit(solution)/shard_map/pallas_call | solution.py:299
  42.7 3.3 %collective-permute-start.4 = (f32[192,128]{1,0:T(8,128)S(1)}, f32[192,128]{1,0:T(8,128)S(1)}, u32[]{:S(2)}, u32[]{:S(2)}) collective-permute-start(f32[192,128]{1,0:T(8,128)S(1)} %shard_map.79), channel_id=1, source_target_pairs={{0,2},{1,3},{2,0},{3,1},{4,6},{5,7},{6,4},{7,5},{8,10},{9,11},{10,... | collective-permute-start | bytes 294920 | tf_op jit(solution)/shard_map/ppermute | solution.py:30
  46.0 1.1 %collective-permute-start.5 = (f32[192,128]{1,0:T(8,128)S(1)}, f32[192,128]{1,0:T(8,128)S(1)}, u32[]{:S(2)}, u32[]{:S(2)}) collective-permute-start(f32[192,128]{1,0:T(8,128)S(1)} %shard_map.79), channel_id=1, source_target_pairs={{0,3},{1,2},{2,1},{3,0},{4,7},{5,6},{6,5},{7,4},{8,11},{9,10},{10,... | collective-permute-start | bytes 294920 | tf_op jit(solution)/shard_map/ppermute | solution.py:30
  47.1 0.0 collective-permute-start.6
  47.1 1.9 %collective-permute-done.4 = f32[192,128]{1,0:T(8,128)S(1)} collective-permute-done((f32[192,128]{1,0:T(8,128)S(1)}, f32[192,128]{1,0:T(8,128)S(1)}, u32[]{:S(2)}, u32[]{:S(2)}) %collective-permute-start.4) | collective-permute-done | bytes 98336 | tf_op jit(solution)/shard_map/ppermute | solution.py:30
  48.9 2.9 %collective-permute-done.5 = f32[192,128]{1,0:T(8,128)S(1)} collective-permute-done((f32[192,128]{1,0:T(8,128)S(1)}, f32[192,128]{1,0:T(8,128)S(1)}, u32[]{:S(2)}, u32[]{:S(2)}) %collective-permute-start.5) | collective-permute-done | bytes 98336 | tf_op jit(solution)/shard_map/ppermute | solution.py:30
  51.8 0.0 collective-permute-done.6
  51.8 0.7 %fusion.9 = (f32[8192]{0:T(1024)}, f32[8192]{0:T(1024)}) fusion(f32[192,128]{1,0:T(8,128)S(1)} %collective-permute-done.6, f32[192,128]{1,0:T(8,128)S(1)} %collective-permute-done.5, f32[192,128]{1,0:T(8,128)S(1)} %collective-permute-done.4, f32[192,128]{1,0:T(8,128)S(1)} %shard_map.79), kind=kLoop, calls=%fused_computation.13 | loop fusion | flops 368640 | bytes 458752 | tf_op jit(solution)/shard_map/reshape | solution.py:358
  (1 shorter events, 0.0 us)
Async XLA Ops:
  0.6 1.0 %copy-start = (f32[4,32768]{1,0:T(4,128)S(1)}, f32[4,32768]{1,0:T(4,128)}, u32[]{:S(2)}) copy-start(f32[4,32768]{1,0:T(4,128)} %param.7) | copy-start | bytes 1572868
  1.7 0.9 %copy-start.1 = (s32[32768]{0:T(1024)S(1)}, s32[32768]{0:T(1024)}, u32[]{:S(2)}) copy-start(s32[32768]{0:T(1024)} %param.8) | copy-start | bytes 393220
  2.6 4.0 %copy-start.2 = (f32[32768]{0:T(1024)S(1)}, f32[32768]{0:T(1024)}, u32[]{:S(2)}) copy-start(f32[32768]{0:T(1024)} %param.9) | copy-start | bytes 393220
  2.6 4.0 %copy-start.3 = (f32[2,8192]{1,0:T(2,128)S(1)}, f32[2,8192]{1,0:T(2,128)}, u32[]{:S(2)}) copy-start(f32[2,8192]{1,0:T(2,128)} %refs_2_.5) | copy-start | bytes 196612
  2.6 4.0 %copy-start.4 = (s32[1,3,2,8]{3,2,1,0:T(2,128)S(1)}, s32[1,3,2,8]{3,2,1,0:T(2,128)}, u32[]{:S(2)}) copy-start(s32[1,3,2,8]{3,2,1,0:T(2,128)} %refs_0_.5) | copy-start | bytes 580
  2.6 3.9 %copy-start.5 = (s32[1,3]{1,0:T(1,128)S(1)}, s32[1,3]{1,0:T(1,128)}, u32[]{:S(2)}) copy-start(s32[1,3]{1,0:T(1,128)} %refs_1_.5) | copy-start | bytes 40
  2.6 15.4 %collective-permute-start = (f32[1280,128]{1,0:T(8,128)S(1)}, f32[1280,128]{1,0:T(8,128)S(1)}, u32[]{:S(2)}, u32[]{:S(2)}) collective-permute-start(f32[1280,128]{1,0:T(8,128)S(1)} %pack.1.refs_4_), channel_id=1, source_target_pairs={{4,8},{8,4},{12,16},{16,12},{20,24},{24,20},{28,32},{32,28},{36,40... | collective-permute-start | bytes 1966088 | tf_op jit(solution)/shard_map/ppermute | solution.py:30
  6.4 11.6 %collective-permute-start.2 = (f32[1280,128]{1,0:T(8,128)S(1)}, f32[1280,128]{1,0:T(8,128)S(1)}, u32[]{:S(2)}, u32[]{:S(2)}) collective-permute-start(f32[1280,128]{1,0:T(8,128)S(1)} %pack.1.refs_4_), channel_id=1, source_target_pairs={{0,4},{4,0},{8,12},{12,8},{16,20},{20,16},{24,28},{28,24},{32,36},... | collective-permute-start | bytes 1966088 | tf_op jit(solution)/shard_map/ppermute | solution.py:30
  18.0 10.9 %collective-permute-start.1 = (f32[1280,128]{1,0:T(8,128)S(1)}, f32[1280,128]{1,0:T(8,128)S(1)}, u32[]{:S(2)}, u32[]{:S(2)}) collective-permute-start(f32[1280,128]{1,0:T(8,128)S(1)} %collective-permute-done.refs_5_), channel_id=1, source_target_pairs={{0,4},{4,0},{8,12},{12,8},{16,20},{20,16},{24,28},{28,24},{32,36},... | collective-permute-start | bytes 1966088 | tf_op jit(solution)/shard_map/ppermute | solution.py:30
  18.0 15.2 %collective-permute-start.3 = (f32[1280,128]{1,0:T(8,128)S(1)}, f32[1280,128]{1,0:T(8,128)S(1)}, u32[]{:S(2)}, u32[]{:S(2)}) collective-permute-start(f32[1280,128]{1,0:T(8,128)S(1)} %collective-permute-done.2.refs_4_), channel_id=1, source_target_pairs={{4,8},{8,4},{12,16},{16,12},{20,24},{24,20},{28,32},{32,28},{36,40... | collective-permute-start | bytes 1966088 | tf_op jit(solution)/shard_map/ppermute | solution.py:30
  42.7 6.2 %collective-permute-start.4 = (f32[192,128]{1,0:T(8,128)S(1)}, f32[192,128]{1,0:T(8,128)S(1)}, u32[]{:S(2)}, u32[]{:S(2)}) collective-permute-start(f32[192,128]{1,0:T(8,128)S(1)} %shard_map.79), channel_id=1, source_target_pairs={{0,2},{1,3},{2,0},{3,1},{4,6},{5,7},{6,4},{7,5},{8,10},{9,11},{10,... | collective-permute-start | bytes 294920 | tf_op jit(solution)/shard_map/ppermute | solution.py:30
  46.0 5.8 %collective-permute-start.5 = (f32[192,128]{1,0:T(8,128)S(1)}, f32[192,128]{1,0:T(8,128)S(1)}, u32[]{:S(2)}, u32[]{:S(2)}) collective-permute-start(f32[192,128]{1,0:T(8,128)S(1)} %shard_map.79), channel_id=1, source_target_pairs={{0,3},{1,2},{2,1},{3,0},{4,7},{5,6},{6,5},{7,4},{8,11},{9,10},{10,... | collective-permute-start | bytes 294920 | tf_op jit(solution)/shard_map/ppermute | solution.py:30
  47.1 4.8 %collective-permute-start.6 = (f32[192,128]{1,0:T(8,128)S(1)}, f32[192,128]{1,0:T(8,128)S(1)}, u32[]{:S(2)}, u32[]{:S(2)}) collective-permute-start(f32[192,128]{1,0:T(8,128)S(1)} %shard_map.79), channel_id=1, source_target_pairs={{0,1},{1,0},{2,3},{3,2},{4,5},{5,4},{6,7},{7,6},{8,9},{9,8},{10,11... | collective-permute-start | bytes 294920 | tf_op jit(solution)/shard_map/ppermute | solution.py:30

commit v2 on v0

--- a/solution.py
+++ b/solution.py
@@ -351,8 +351,9 @@
     part = join(1, *args, near1, far1, part)
     part = join(2, *args, near2, far2, part)
     state = unpack(part)
-    for flip in (1, 3, 2):
-        state = combine(state, unpack(swapped(part, "poly", lambda q: q ^ flip)))
+    for flip in (2, 3, 1):
+        theirs = swapped(part, "poly", lambda q: q ^ flip)
+        state = combine(state, unpack(theirs))
     state = combine(state, (FAR, 1.0, 0.0))
     return (state[0] * (1.0 / SCALE)).reshape(-1), (state[2] / state[1]).reshape(-1)
 

time: 53.3 us -> 52.5 us (0.985)
  waiting for transfers between devices: 14.2 us -> 13.6 us
    ppermute x7, waiting for transfers between devices: 14.2 us -> 13.6 us  [swapped(): return lax.ppermute(shard, axis, pairs)]
  transfers between devices with their start and end apart: 7 -> 7, of which waited for: 5 -> 4; matrix products, arithmetic and copies ran while one was open for 0% -> 0% of each run, Pallas kernels for 27% -> 27%
where the time goes in v2:
time: 52.5 us; the launch traced here: 52.3 us
  Pallas kernels  23.4 us (45%)
  waiting for transfers between devices  13.6 us (26%)
  starting transfers between devices  11.9 us (23%)
  local copies, waits for them, and re-layouts  1.96 us (4%)
  between operations  0.75 us (1%)
  other arithmetic  0.7 us (1%)
    pallas_call x3, Pallas kernels, join(): pl.pallas_call(body, out_shape=jax.ShapeDtypeStruct((192, 128), f32), in_...  23.3 us
    ppermute x7, waiting for transfers between devices, swapped(): return lax.ppermute(shard, axis, pairs)  13.6 us
    ppermute x7, starting transfers between devices, swapped(): return lax.ppermute(shard, axis, pairs)  11.9 us
    unnamed x12, local copies, waits for them, and re-layouts  1.96 us
  transfers between devices with their start and end apart: 7, of which 4 were waited for; matrix products, arithmetic and copies ran while one was open for 0% of the time, Pallas kernels for 27%

profile of v2, /device:TPU:128, one launch (start us, length us, event | category | flops | bytes accessed | tf_op | source)
XLA Modules:
  0.0 52.3 jit_solution(8435016037779837908)
XLA Ops:
  0.6 0.0 copy-start
  0.6 1.0 %copy-done = f32[4,32768]{1,0:T(4,128)S(1)} copy-done((f32[4,32768]{1,0:T(4,128)S(1)}, f32[4,32768]{1,0:T(4,128)}, u32[]{:S(2)}) %copy-start) | copy-done | bytes 524312
  1.7 0.0 copy-start.1
  1.7 0.9 %copy-done.1 = s32[32768]{0:T(1024)S(1)} copy-done((s32[32768]{0:T(1024)S(1)}, s32[32768]{0:T(1024)}, u32[]{:S(2)}) %copy-start.1) | copy-done | bytes 131096
  2.6 0.0 copy-start.2
  2.6 0.0 copy-start.3
  2.6 0.0 copy-start.4
  2.6 0.0 copy-start.5
  2.6 3.8 %collective-permute-start = (f32[1280,128]{1,0:T(8,128)S(1)}, f32[1280,128]{1,0:T(8,128)S(1)}, u32[]{:S(2)}, u32[]{:S(2)}) collective-permute-start(f32[1280,128]{1,0:T(8,128)S(1)} %pack.1.refs_4_), channel_id=1, source_target_pairs={{4,8},{8,4},{12,16},{16,12},{20,24},{24,20},{28,32},{32,28},{36,40... | collective-permute-start | bytes 1966088 | tf_op jit(solution)/shard_map/ppermute | solution.py:30
  6.4 0.1 collective-permute-start.2
  6.5 0.0 copy-done.2
  6.5 0.0 copy-done.3
  6.6 0.0 copy-done.4
  6.6 0.0 copy-done.5
  6.6 7.1 %shard_map.77.refs_6_ = f32[192,128]{1,0:T(8,128)S(1)} custom-call(s32[1,3,2,8]{3,2,1,0:T(2,128)S(1)} %copy-done.4, s32[1,3]{1,0:T(1,128)S(1)} %copy-done.5, f32[2,8192]{1,0:T(2,128)S(1)} %copy-done.3, f32[256,128]{1,0:T(8,128)S(1)} %bitcast.13, f32[1280,128]{1,0:T(8,128)S(1)} %pack.1.refs_4_), custom_call_target="tpu_custom_call" | custom-call | flops 83886080 | bytes 1048576 | tf_op jit(solution)/shard_map/pallas_call | solution.py:299
  13.7 4.3 %collective-permute-done.refs_5_ = f32[1280,128]{1,0:T(8,128)S(1)} collective-permute-done((f32[1280,128]{1,0:T(8,128)S(1)}, f32[1280,128]{1,0:T(8,128)S(1)}, u32[]{:S(2)}, u32[]{:S(2)}) %collective-permute-start) | collective-permute-done | bytes 655392 | tf_op jit(solution)/shard_map/ppermute | solution.py:30
  18.0 0.0 collective-permute-start.1
  18.0 0.0 collective-permute-done.2.refs_4_
  18.0 3.6 %collective-permute-start.3 = (f32[1280,128]{1,0:T(8,128)S(1)}, f32[1280,128]{1,0:T(8,128)S(1)}, u32[]{:S(2)}, u32[]{:S(2)}) collective-permute-start(f32[1280,128]{1,0:T(8,128)S(1)} %collective-permute-done.2.refs_4_), channel_id=1, source_target_pairs={{4,8},{8,4},{12,16},{16,12},{20,24},{24,20},{28,32},{32,28},{36,40... | collective-permute-start | bytes 1966088 | tf_op jit(solution)/shard_map/ppermute | solution.py:30
  21.7 7.0 %shard_map.78.refs_6_ = f32[192,128]{1,0:T(8,128)S(1)} custom-call(s32[1,3,2,8]{3,2,1,0:T(2,128)S(1)} %copy-done.4, s32[1,3]{1,0:T(1,128)S(1)} %copy-done.5, f32[2,8192]{1,0:T(2,128)S(1)} %copy-done.3, f32[256,128]{1,0:T(8,128)S(1)} %bitcast.14, f32[1280,128]{1,0:T(8,128)S(1)} %collective-permute-done.2.refs_4_, ...), custom_call_target="tpu_custom_call" | custom-call | flops 83886080 | bytes 1048576 | tf_op jit(solution)/shard_map/pallas_call | solution.py:299
  28.7 0.0 collective-permute-done.1.refs_4_
  28.7 4.5 %collective-permute-done.3.refs_5_ = f32[1280,128]{1,0:T(8,128)S(1)} collective-permute-done((f32[1280,128]{1,0:T(8,128)S(1)}, f32[1280,128]{1,0:T(8,128)S(1)}, u32[]{:S(2)}, u32[]{:S(2)}) %collective-permute-start.3) | collective-permute-done | bytes 655392 | tf_op jit(solution)/shard_map/ppermute | solution.py:30
  33.2 9.2 %shard_map.79 = f32[192,128]{1,0:T(8,128)S(1)} custom-call(s32[1,3,2,8]{3,2,1,0:T(2,128)S(1)} %copy-done.4, s32[1,3]{1,0:T(1,128)S(1)} %copy-done.5, f32[2,8192]{1,0:T(2,128)S(1)} %copy-done.3, f32[256,128]{1,0:T(8,128)S(1)} %bitcast.15, f32[1280,128]{1,0:T(8,128)S(1)} %collective-permute-done.1.refs_4_, f32[1280,128]{1,0:T(8,128)S(1)} %collective-permute-done.3.refs_5_, ...), custom_call_target="tpu_custom_call" | custom-call | flops 83886080 | bytes 1048576 | tf_op jit(solution)/shard_map/pallas_call | solution.py:299
  42.5 3.3 %collective-permute-start.4 = (f32[192,128]{1,0:T(8,128)S(1)}, f32[192,128]{1,0:T(8,128)S(1)}, u32[]{:S(2)}, u32[]{:S(2)}) collective-permute-start(f32[192,128]{1,0:T(8,128)S(1)} %shard_map.79), channel_id=1, source_target_pairs={{0,2},{1,3},{2,0},{3,1},{4,6},{5,7},{6,4},{7,5},{8,10},{9,11},{10,... | collective-permute-start | bytes 294920 | tf_op jit(solution)/shard_map/ppermute | solution.py:30
  45.7 1.0 %collective-permute-start.5 = (f32[192,128]{1,0:T(8,128)S(1)}, f32[192,128]{1,0:T(8,128)S(1)}, u32[]{:S(2)}, u32[]{:S(2)}) collective-permute-start(f32[192,128]{1,0:T(8,128)S(1)} %shard_map.79), channel_id=1, source_target_pairs={{0,3},{1,2},{2,1},{3,0},{4,7},{5,6},{6,5},{7,4},{8,11},{9,10},{10,... | collective-permute-start | bytes 294920 | tf_op jit(solution)/shard_map/ppermute | solution.py:30
  46.8 0.0 collective-permute-start.6
  46.8 1.9 %collective-permute-done.4 = f32[192,128]{1,0:T(8,128)S(1)} collective-permute-done((f32[192,128]{1,0:T(8,128)S(1)}, f32[192,128]{1,0:T(8,128)S(1)}, u32[]{:S(2)}, u32[]{:S(2)}) %collective-permute-start.4) | collective-permute-done | bytes 98336 | tf_op jit(solution)/shard_map/ppermute | solution.py:30
  48.7 2.9 %collective-permute-done.5 = f32[192,128]{1,0:T(8,128)S(1)} collective-permute-done((f32[192,128]{1,0:T(8,128)S(1)}, f32[192,128]{1,0:T(8,128)S(1)}, u32[]{:S(2)}, u32[]{:S(2)}) %collective-permute-start.5) | collective-permute-done | bytes 98336 | tf_op jit(solution)/shard_map/ppermute | solution.py:30
  51.6 0.0 collective-permute-done.6
  51.6 0.7 %fusion.9 = (f32[8192]{0:T(1024)}, f32[8192]{0:T(1024)}) fusion(f32[192,128]{1,0:T(8,128)S(1)} %collective-permute-done.6, f32[192,128]{1,0:T(8,128)S(1)} %collective-permute-done.5, f32[192,128]{1,0:T(8,128)S(1)} %collective-permute-done.4, f32[192,128]{1,0:T(8,128)S(1)} %shard_map.79), kind=kLoop, calls=%fused_computation.13 | loop fusion | flops 368640 | bytes 458752 | tf_op jit(solution)/shard_map/reshape | solution.py:358
  (1 shorter events, 0.0 us)
Async XLA Ops:
  0.6 1.0 %copy-start = (f32[4,32768]{1,0:T(4,128)S(1)}, f32[4,32768]{1,0:T(4,128)}, u32[]{:S(2)}) copy-start(f32[4,32768]{1,0:T(4,128)} %param.7) | copy-start | bytes 1572868
  1.7 0.9 %copy-start.1 = (s32[32768]{0:T(1024)S(1)}, s32[32768]{0:T(1024)}, u32[]{:S(2)}) copy-start(s32[32768]{0:T(1024)} %param.8) | copy-start | bytes 393220
  2.6 4.0 %copy-start.2 = (f32[32768]{0:T(1024)S(1)}, f32[32768]{0:T(1024)}, u32[]{:S(2)}) copy-start(f32[32768]{0:T(1024)} %param.9) | copy-start | bytes 393220
  2.6 4.0 %copy-start.3 = (f32[2,8192]{1,0:T(2,128)S(1)}, f32[2,8192]{1,0:T(2,128)}, u32[]{:S(2)}) copy-start(f32[2,8192]{1,0:T(2,128)} %refs_2_.5) | copy-start | bytes 196612
  2.6 4.0 %copy-start.4 = (s32[1,3,2,8]{3,2,1,0:T(2,128)S(1)}, s32[1,3,2,8]{3,2,1,0:T(2,128)}, u32[]{:S(2)}) copy-start(s32[1,3,2,8]{3,2,1,0:T(2,128)} %refs_0_.5) | copy-start | bytes 580
  2.6 3.9 %copy-start.5 = (s32[1,3]{1,0:T(1,128)S(1)}, s32[1,3]{1,0:T(1,128)}, u32[]{:S(2)}) copy-start(s32[1,3]{1,0:T(1,128)} %refs_1_.5) | copy-start | bytes 40
  2.6 15.4 %collective-permute-start = (f32[1280,128]{1,0:T(8,128)S(1)}, f32[1280,128]{1,0:T(8,128)S(1)}, u32[]{:S(2)}, u32[]{:S(2)}) collective-permute-start(f32[1280,128]{1,0:T(8,128)S(1)} %pack.1.refs_4_), channel_id=1, source_target_pairs={{4,8},{8,4},{12,16},{16,12},{20,24},{24,20},{28,32},{32,28},{36,40... | collective-permute-start | bytes 1966088 | tf_op jit(solution)/shard_map/ppermute | solution.py:30
  6.4 11.6 %collective-permute-start.2 = (f32[1280,128]{1,0:T(8,128)S(1)}, f32[1280,128]{1,0:T(8,128)S(1)}, u32[]{:S(2)}, u32[]{:S(2)}) collective-permute-start(f32[1280,128]{1,0:T(8,128)S(1)} %pack.1.refs_4_), channel_id=1, source_target_pairs={{0,4},{4,0},{8,12},{12,8},{16,20},{20,16},{24,28},{28,24},{32,36},... | collective-permute-start | bytes 1966088 | tf_op jit(solution)/shard_map/ppermute | solution.py:30
  18.0 10.7 %collective-permute-start.1 = (f32[1280,128]{1,0:T(8,128)S(1)}, f32[1280,128]{1,0:T(8,128)S(1)}, u32[]{:S(2)}, u32[]{:S(2)}) collective-permute-start(f32[1280,128]{1,0:T(8,128)S(1)} %collective-permute-done.refs_5_), channel_id=1, source_target_pairs={{0,4},{4,0},{8,12},{12,8},{16,20},{20,16},{24,28},{28,24},{32,36},... | collective-permute-start | bytes 1966088 | tf_op jit(solution)/shard_map/ppermute | solution.py:30
  18.0 15.2 %collective-permute-start.3 = (f32[1280,128]{1,0:T(8,128)S(1)}, f32[1280,128]{1,0:T(8,128)S(1)}, u32[]{:S(2)}, u32[]{:S(2)}) collective-permute-start(f32[1280,128]{1,0:T(8,128)S(1)} %collective-permute-done.2.refs_4_), channel_id=1, source_target_pairs={{4,8},{8,4},{12,16},{16,12},{20,24},{24,20},{28,32},{32,28},{36,40... | collective-permute-start | bytes 1966088 | tf_op jit(solution)/shard_map/ppermute | solution.py:30
  42.5 6.2 %collective-permute-start.4 = (f32[192,128]{1,0:T(8,128)S(1)}, f32[192,128]{1,0:T(8,128)S(1)}, u32[]{:S(2)}, u32[]{:S(2)}) collective-permute-start(f32[192,128]{1,0:T(8,128)S(1)} %shard_map.79), channel_id=1, source_target_pairs={{0,2},{1,3},{2,0},{3,1},{4,6},{5,7},{6,4},{7,5},{8,10},{9,11},{10,... | collective-permute-start | bytes 294920 | tf_op jit(solution)/shard_map/ppermute | solution.py:30
  45.7 5.8 %collective-permute-start.5 = (f32[192,128]{1,0:T(8,128)S(1)}, f32[192,128]{1,0:T(8,128)S(1)}, u32[]{:S(2)}, u32[]{:S(2)}) collective-permute-start(f32[192,128]{1,0:T(8,128)S(1)} %shard_map.79), channel_id=1, source_target_pairs={{0,3},{1,2},{2,1},{3,0},{4,7},{5,6},{6,5},{7,4},{8,11},{9,10},{10,... | collective-permute-start | bytes 294920 | tf_op jit(solution)/shard_map/ppermute | solution.py:30
  46.8 4.8 %collective-permute-start.6 = (f32[192,128]{1,0:T(8,128)S(1)}, f32[192,128]{1,0:T(8,128)S(1)}, u32[]{:S(2)}, u32[]{:S(2)}) collective-permute-start(f32[192,128]{1,0:T(8,128)S(1)} %shard_map.79), channel_id=1, source_target_pairs={{0,1},{1,0},{2,3},{3,2},{4,5},{5,4},{6,7},{7,6},{8,9},{9,8},{10,11... | collective-permute-start | bytes 294920 | tf_op jit(solution)/shard_map/ppermute | solution.py:30

commit v3 on v2

--- a/solution.py
+++ b/solution.py
@@ -30,9 +30,14 @@
     return lax.ppermute(shard, axis, pairs)
 
 
-def pack_kernel(corners, polygons, out):
-    out[0:1024, :] = corners[...]
-    out[1024:1280, :] = polygons[...].astype(jnp.float32)
+def pack_kernel(corners, polygons, out, names, sems):
+    first = pltpu.make_async_copy(corners, out.at[pl.ds(0, 1024), :], sems.at[0])
+    second = pltpu.make_async_copy(polygons, names, sems.at[1])
+    first.start()
+    second.start()
+    second.wait()
+    out[1024:1280, :] = names[...].astype(jnp.float32)
+    first.wait()
 
 
 def packed_cell(segments, edge_polygon):
@@ -40,12 +45,13 @@
     return pl.pallas_call(
         pack_kernel,
         out_shape=jax.ShapeDtypeStruct((1280, 128), jnp.float32),
-        in_specs=[VMEM] * 2,
+        in_specs=[pl.BlockSpec(memory_space=pltpu.HBM)] * 2,
         out_specs=VMEM,
+        scratch_shapes=[pltpu.VMEM((256, 128), jnp.int32), pltpu.SemaphoreType.DMA((2,))],
         compiler_params=pltpu.CompilerParams(vmem_limit_bytes=4 << 20),
         cost_estimate=pl.CostEstimate(flops=1 << 20, bytes_accessed=1 << 21, transcendentals=0),
         name="pack",
-    )(corners, edge_polygon.reshape(-1, 128))
+    )(*(pltpu.with_memory_space_constraint(x, pltpu.HBM) for x in (corners, edge_polygon.reshape(-1, 128))))
 
 
 def pieces(x):

time: 52.5 us -> 51.5 us (0.981)
  local copies, waits for them, and re-layouts: 1.96 us -> 0.02 us
  Pallas kernels: 23.4 us -> 24.5 us
    unnamed x12 -> x8, local copies, waits for them, and re-layouts: 1.96 us -> 0.02 us
    pallas_call x1, Pallas kernels: 0.04 us -> 1.13 us  [packed_cell(): pl.pallas_call(pack_kernel, out_shape=jax.ShapeDtypeStruct((1280, 128), j...]
  transfers between devices with their start and end apart: 7 -> 7, of which waited for: 4 -> 4; matrix products, arithmetic and copies ran while one was open for 0% -> 0% of each run, Pallas kernels for 27% -> 28%
where the time goes in v3:
time: 51.5 us; the launch traced here: 51.3 us
  Pallas kernels  24.5 us (48%)
  waiting for transfers between devices  13.6 us (26%)
  starting transfers between devices  11.7 us (23%)
  between operations  0.76 us (1%)
  other arithmetic  0.7 us (1%)
    pallas_call x3, Pallas kernels, join(): pl.pallas_call(body, out_shape=jax.ShapeDtypeStruct((192, 128), f32), in_...  23.4 us
    ppermute x7, waiting for transfers between devices, swapped(): return lax.ppermute(shard, axis, pairs)  13.6 us
    ppermute x7, starting transfers between devices, swapped(): return lax.ppermute(shard, axis, pairs)  11.7 us
    pallas_call x1, Pallas kernels, packed_cell(): pl.pallas_call(pack_kernel, out_shape=jax.ShapeDtypeStruct((1280, 128), j...  1.13 us
  transfers between devices with their start and end apart: 7, of which 4 were waited for; matrix products, arithmetic and copies ran while one was open for 0% of the time, Pallas kernels for 28%

profile of v3, /device:TPU:128, one launch (start us, length us, event | category | flops | bytes accessed | tf_op | source)
XLA Modules:
  0.0 51.3 jit_solution(237174198343614347)
XLA Ops:
  0.6 0.0 copy-start
  0.6 0.0 copy-start.1
  0.7 0.0 copy-start.2
  0.7 1.1 %pack.1.refs_4_ = f32[1280,128]{1,0:T(8,128)S(1)} custom-call(f32[1024,128]{1,0:T(8,128)} %bitcast.14, s32[256,128]{1,0:T(8,128)} %bitcast.15), custom_call_target="tpu_custom_call" | custom-call | flops 1048576 | bytes 2097152 | tf_op jit(solution)/shard_map/pack/pallas_call | solution.py:45
  1.8 0.0 copy-start.3
  1.8 3.7 %collective-permute-start = (f32[1280,128]{1,0:T(8,128)S(1)}, f32[1280,128]{1,0:T(8,128)S(1)}, u32[]{:S(2)}, u32[]{:S(2)}) collective-permute-start(f32[1280,128]{1,0:T(8,128)S(1)} %pack.1.refs_4_), channel_id=1, source_target_pairs={{4,8},{8,4},{12,16},{16,12},{20,24},{24,20},{28,32},{32,28},{36,40... | collective-permute-start | bytes 1966088 | tf_op jit(solution)/shard_map/ppermute | solution.py:30
  5.5 0.1 collective-permute-start.2
  5.6 0.0 copy-done
  5.6 0.0 copy-done.1
  5.6 0.0 copy-done.2
  5.6 0.0 copy-done.3
  5.6 7.1 %shard_map.77.refs_6_ = f32[192,128]{1,0:T(8,128)S(1)} custom-call(s32[1,3,2,8]{3,2,1,0:T(2,128)S(1)} %copy-done.2, s32[1,3]{1,0:T(1,128)S(1)} %copy-done.3, f32[2,8192]{1,0:T(2,128)S(1)} %copy-done.1, f32[256,128]{1,0:T(8,128)S(1)} %bitcast.11, f32[1280,128]{1,0:T(8,128)S(1)} %pack.1.refs_4_), custom_call_target="tpu_custom_call" | custom-call | flops 83886080 | bytes 1048576 | tf_op jit(solution)/shard_map/pallas_call | solution.py:305
  12.7 4.3 %collective-permute-done.refs_5_ = f32[1280,128]{1,0:T(8,128)S(1)} collective-permute-done((f32[1280,128]{1,0:T(8,128)S(1)}, f32[1280,128]{1,0:T(8,128)S(1)}, u32[]{:S(2)}, u32[]{:S(2)}) %collective-permute-start) | collective-permute-done | bytes 655392 | tf_op jit(solution)/shard_map/ppermute | solution.py:30
  17.0 0.0 collective-permute-start.1
  17.0 0.0 collective-permute-done.2.refs_4_
  17.0 3.6 %collective-permute-start.3 = (f32[1280,128]{1,0:T(8,128)S(1)}, f32[1280,128]{1,0:T(8,128)S(1)}, u32[]{:S(2)}, u32[]{:S(2)}) collective-permute-start(f32[1280,128]{1,0:T(8,128)S(1)} %collective-permute-done.2.refs_4_), channel_id=1, source_target_pairs={{4,8},{8,4},{12,16},{16,12},{20,24},{24,20},{28,32},{32,28},{36,40... | collective-permute-start | bytes 1966088 | tf_op jit(solution)/shard_map/ppermute | solution.py:30
  20.7 7.0 %shard_map.78.refs_6_ = f32[192,128]{1,0:T(8,128)S(1)} custom-call(s32[1,3,2,8]{3,2,1,0:T(2,128)S(1)} %copy-done.2, s32[1,3]{1,0:T(1,128)S(1)} %copy-done.3, f32[2,8192]{1,0:T(2,128)S(1)} %copy-done.1, f32[256,128]{1,0:T(8,128)S(1)} %bitcast.12, f32[1280,128]{1,0:T(8,128)S(1)} %collective-permute-done.2.refs_4_, ...), custom_call_target="tpu_custom_call" | custom-call | flops 83886080 | bytes 1048576 | tf_op jit(solution)/shard_map/pallas_call | solution.py:305
  27.7 0.0 collective-permute-done.1.refs_4_
  27.7 4.5 %collective-permute-done.3.refs_5_ = f32[1280,128]{1,0:T(8,128)S(1)} collective-permute-done((f32[1280,128]{1,0:T(8,128)S(1)}, f32[1280,128]{1,0:T(8,128)S(1)}, u32[]{:S(2)}, u32[]{:S(2)}) %collective-permute-start.3) | collective-permute-done | bytes 655392 | tf_op jit(solution)/shard_map/ppermute | solution.py:30
  32.3 9.2 %shard_map.79 = f32[192,128]{1,0:T(8,128)S(1)} custom-call(s32[1,3,2,8]{3,2,1,0:T(2,128)S(1)} %copy-done.2, s32[1,3]{1,0:T(1,128)S(1)} %copy-done.3, f32[2,8192]{1,0:T(2,128)S(1)} %copy-done.1, f32[256,128]{1,0:T(8,128)S(1)} %bitcast.13, f32[1280,128]{1,0:T(8,128)S(1)} %collective-permute-done.1.refs_4_, f32[1280,128]{1,0:T(8,128)S(1)} %collective-permute-done.3.refs_5_, ...), custom_call_target="tpu_custom_call" | custom-call | flops 83886080 | bytes 1048576 | tf_op jit(solution)/shard_map/pallas_call | solution.py:305
  41.5 3.3 %collective-permute-start.4 = (f32[192,128]{1,0:T(8,128)S(1)}, f32[192,128]{1,0:T(8,128)S(1)}, u32[]{:S(2)}, u32[]{:S(2)}) collective-permute-start(f32[192,128]{1,0:T(8,128)S(1)} %shard_map.79), channel_id=1, source_target_pairs={{0,2},{1,3},{2,0},{3,1},{4,6},{5,7},{6,4},{7,5},{8,10},{9,11},{10,... | collective-permute-start | bytes 294920 | tf_op jit(solution)/shard_map/ppermute | solution.py:30
  44.8 1.1 %collective-permute-start.5 = (f32[192,128]{1,0:T(8,128)S(1)}, f32[192,128]{1,0:T(8,128)S(1)}, u32[]{:S(2)}, u32[]{:S(2)}) collective-permute-start(f32[192,128]{1,0:T(8,128)S(1)} %shard_map.79), channel_id=1, source_target_pairs={{0,3},{1,2},{2,1},{3,0},{4,7},{5,6},{6,5},{7,4},{8,11},{9,10},{10,... | collective-permute-start | bytes 294920 | tf_op jit(solution)/shard_map/ppermute | solution.py:30
  45.8 0.0 collective-permute-start.6
  45.8 1.9 %collective-permute-done.4 = f32[192,128]{1,0:T(8,128)S(1)} collective-permute-done((f32[192,128]{1,0:T(8,128)S(1)}, f32[192,128]{1,0:T(8,128)S(1)}, u32[]{:S(2)}, u32[]{:S(2)}) %collective-permute-start.4) | collective-permute-done | bytes 98336 | tf_op jit(solution)/shard_map/ppermute | solution.py:30
  47.7 2.9 %collective-permute-done.5 = f32[192,128]{1,0:T(8,128)S(1)} collective-permute-done((f32[192,128]{1,0:T(8,128)S(1)}, f32[192,128]{1,0:T(8,128)S(1)}, u32[]{:S(2)}, u32[]{:S(2)}) %collective-permute-start.5) | collective-permute-done | bytes 98336 | tf_op jit(solution)/shard_map/ppermute | solution.py:30
  50.6 0.0 collective-permute-done.6
  50.6 0.7 %fusion.9 = (f32[8192]{0:T(1024)}, f32[8192]{0:T(1024)}) fusion(f32[192,128]{1,0:T(8,128)S(1)} %collective-permute-done.6, f32[192,128]{1,0:T(8,128)S(1)} %collective-permute-done.5, f32[192,128]{1,0:T(8,128)S(1)} %collective-permute-done.4, f32[192,128]{1,0:T(8,128)S(1)} %shard_map.79), kind=kLoop, calls=%fused_computation.13 | loop fusion | flops 368640 | bytes 458752 | tf_op jit(solution)/shard_map/reshape | solution.py:364
Async XLA Ops:
  0.6 4.9 %copy-start = (f32[32768]{0:T(1024)S(1)}, f32[32768]{0:T(1024)}, u32[]{:S(2)}) copy-start(f32[32768]{0:T(1024)} %param.9) | copy-start | bytes 393220
  0.6 4.9 %copy-start.1 = (f32[2,8192]{1,0:T(2,128)S(1)}, f32[2,8192]{1,0:T(2,128)}, u32[]{:S(2)}) copy-start(f32[2,8192]{1,0:T(2,128)} %refs_2_.5) | copy-start | bytes 196612
  0.7 4.9 %copy-start.2 = (s32[1,3,2,8]{3,2,1,0:T(2,128)S(1)}, s32[1,3,2,8]{3,2,1,0:T(2,128)}, u32[]{:S(2)}) copy-start(s32[1,3,2,8]{3,2,1,0:T(2,128)} %refs_0_.5) | copy-start | bytes 580
  1.8 3.8 %copy-start.3 = (s32[1,3]{1,0:T(1,128)S(1)}, s32[1,3]{1,0:T(1,128)}, u32[]{:S(2)}) copy-start(s32[1,3]{1,0:T(1,128)} %refs_1_.5) | copy-start | bytes 40
  1.8 15.2 %collective-permute-start = (f32[1280,128]{1,0:T(8,128)S(1)}, f32[1280,128]{1,0:T(8,128)S(1)}, u32[]{:S(2)}, u32[]{:S(2)}) collective-permute-start(f32[1280,128]{1,0:T(8,128)S(1)} %pack.1.refs_4_), channel_id=1, source_target_pairs={{4,8},{8,4},{12,16},{16,12},{20,24},{24,20},{28,32},{32,28},{36,40... | collective-permute-start | bytes 1966088 | tf_op jit(solution)/shard_map/ppermute | solution.py:30
  5.5 11.6 %collective-permute-start.2 = (f32[1280,128]{1,0:T(8,128)S(1)}, f32[1280,128]{1,0:T(8,128)S(1)}, u32[]{:S(2)}, u32[]{:S(2)}) collective-permute-start(f32[1280,128]{1,0:T(8,128)S(1)} %pack.1.refs_4_), channel_id=1, source_target_pairs={{0,4},{4,0},{8,12},{12,8},{16,20},{20,16},{24,28},{28,24},{32,36},... | collective-permute-start | bytes 1966088 | tf_op jit(solution)/shard_map/ppermute | solution.py:30
  17.0 10.7 %collective-permute-start.1 = (f32[1280,128]{1,0:T(8,128)S(1)}, f32[1280,128]{1,0:T(8,128)S(1)}, u32[]{:S(2)}, u32[]{:S(2)}) collective-permute-start(f32[1280,128]{1,0:T(8,128)S(1)} %collective-permute-done.refs_5_), channel_id=1, source_target_pairs={{0,4},{4,0},{8,12},{12,8},{16,20},{20,16},{24,28},{28,24},{32,36},... | collective-permute-start | bytes 1966088 | tf_op jit(solution)/shard_map/ppermute | solution.py:30
  17.0 15.2 %collective-permute-start.3 = (f32[1280,128]{1,0:T(8,128)S(1)}, f32[1280,128]{1,0:T(8,128)S(1)}, u32[]{:S(2)}, u32[]{:S(2)}) collective-permute-start(f32[1280,128]{1,0:T(8,128)S(1)} %collective-permute-done.2.refs_4_), channel_id=1, source_target_pairs={{4,8},{8,4},{12,16},{16,12},{20,24},{24,20},{28,32},{32,28},{36,40... | collective-permute-start | bytes 1966088 | tf_op jit(solution)/shard_map/ppermute | solution.py:30
  41.5 6.2 %collective-permute-start.4 = (f32[192,128]{1,0:T(8,128)S(1)}, f32[192,128]{1,0:T(8,128)S(1)}, u32[]{:S(2)}, u32[]{:S(2)}) collective-permute-start(f32[192,128]{1,0:T(8,128)S(1)} %shard_map.79), channel_id=1, source_target_pairs={{0,2},{1,3},{2,0},{3,1},{4,6},{5,7},{6,4},{7,5},{8,10},{9,11},{10,... | collective-permute-start | bytes 294920 | tf_op jit(solution)/shard_map/ppermute | solution.py:30
  44.8 5.8 %collective-permute-start.5 = (f32[192,128]{1,0:T(8,128)S(1)}, f32[192,128]{1,0:T(8,128)S(1)}, u32[]{:S(2)}, u32[]{:S(2)}) collective-permute-start(f32[192,128]{1,0:T(8,128)S(1)} %shard_map.79), channel_id=1, source_target_pairs={{0,3},{1,2},{2,1},{3,0},{4,7},{5,6},{6,5},{7,4},{8,11},{9,10},{10,... | collective-permute-start | bytes 294920 | tf_op jit(solution)/shard_map/ppermute | solution.py:30
  45.8 4.8 %collective-permute-start.6 = (f32[192,128]{1,0:T(8,128)S(1)}, f32[192,128]{1,0:T(8,128)S(1)}, u32[]{:S(2)}, u32[]{:S(2)}) collective-permute-start(f32[192,128]{1,0:T(8,128)S(1)} %shard_map.79), channel_id=1, source_target_pairs={{0,1},{1,0},{2,3},{3,2},{4,5},{5,4},{6,7},{7,6},{8,9},{9,8},{10,11... | collective-permute-start | bytes 294920 | tf_op jit(solution)/shard_map/ppermute | solution.py:30
